TPU v7x, 32 devices: a whole 2x2x4 slice. The times are simulated.
32 devices in a mesh: groups: 2 (over x), box: 16 (over z, y, core).
Axes of the slice: x: 2, y: 2, z: 4, core: 2. Of those that a mesh axis runs over, the one named last changes fastest.
Arguments:
- right_sides: float32 [128, 256, 384], P(('groups', 'box')), parts along dimension 0, may hold values from -6 to 6
- blocks: bfloat16 [128, 4, 4, 256, 256], P(('groups', 'box')), parts along dimension 0, may hold values from -0.1875 to 0.1875
- contrast: float32 [8192], P(('groups', 'box')), parts along dimension 0, may hold values from 0.3 to 3
- sample_index: int32 [64, 256], P('box'), may hold values from 0 to 4095
- owners: int32 [64, 4, 4], P('box'), may hold values from 0 to 3, each once within a row
Outputs:
- scattered: float32 [128, 256, 384], P(('groups', 'box')), parts along dimension 0
There are 2 independent parts, one for each index of `groups`. A program takes and returns all parts, laid end to end along the dimension named above; an argument that names none is the same for every part. Nothing has to cross between parts.
Inputs may be any that keep to these rules, and one draw needn't show every extreme that they name: Each row owners[b, m, :] holds every value 0 to 3 once.
All inputs are finite; a program needn't handle non-finite values.
Results may differ from a plain program's by a relative error of at most 0.0093.
Values may be sent and summed in bfloat16 or wider, within the bound.
No kernel may reach another device: no remote copies, remote signals or barrier semaphores. Data moves between devices by JAX's collectives and lax.ppermute only.
A program may use at most 128 MiB of HBM per device.

v0:
```python
import jax
import jax.numpy as jnp
from jax import lax
from jax.sharding import PartitionSpec as P


def partner(x, axis, distance):
    return lax.ppermute(x, axis, [(i, i ^ 1 << distance) for i in range(lax.axis_size(axis))])


def collect(rounded, first_bit, second_bit):
    position = lax.axis_index("box")
    remote = partner(rounded, "box", first_bit)
    first_value = position >> first_bit & 1
    lower = jnp.where(first_value == 0, rounded, remote)
    upper = jnp.where(first_value == 0, remote, rounded)
    pair_rows = jnp.stack([lower, upper])
    other_pair = partner(pair_rows, "box", second_bit)
    second_value = position >> second_bit & 1
    whole = jnp.where(
        second_value == 0, jnp.stack([pair_rows, other_pair]), jnp.stack([other_pair, pair_rows])
    )
    return whole.reshape((4,) + rounded.shape)


def spread(pieces, first_bit, second_bit):
    position = lax.axis_index("box")
    grid = pieces.reshape((2, 2) + pieces.shape[1:])
    grid = jnp.swapaxes(grid, 0, 1)
    first_value = position >> first_bit & 1
    kept_half = jnp.where(first_value == 0, grid[0], grid[1])
    sent_half = jnp.where(first_value == 0, grid[1], grid[0])
    partial_value = kept_half + partner(sent_half, "box", first_bit)
    second_value = position >> second_bit & 1
    kept_piece = jnp.where(second_value == 0, partial_value[0], partial_value[1])
    sent_piece = jnp.where(second_value == 0, partial_value[1], partial_value[0])
    return kept_piece + partner(sent_piece, "box", second_bit)


def section_bits(layer_index, digit_count):
    low_bit = 2 * ((layer_index - 1) % digit_count)
    high_bit = low_bit + 1
    return (low_bit, high_bit)


def per_device(right_sides, blocks, contrast, sample_index, owners):
    contrast_lookup = lax.all_gather(contrast, "box", axis=0, tiled=True)
    digit_count = (lax.axis_size("box").bit_length() - 1) // 2
    resident_boxes = right_sides.shape[0]
    slots = jnp.arange(4, dtype=jnp.int32)
    current = right_sides
    for layer_index in range(blocks.shape[1]):
        rounded = current.astype(jnp.bfloat16)
        if layer_index == 0:
            gathered_groups = jnp.broadcast_to(rounded[None], (resident_boxes,) + rounded.shape)
        else:
            first_bit, second_bit = section_bits(layer_index, digit_count)
            gathered_groups = jnp.swapaxes(collect(rounded, first_bit, second_bit), 0, 1)
        owner_row = owners[:, layer_index, :]
        inverse = jnp.sum(
            (owner_row[:, :, None] == slots[None, None, :]).astype(jnp.int32)
            * slots[None, :, None],
            axis=1,
        )
        selected_rows = jnp.take_along_axis(gathered_groups, inverse[:, :, None, None], axis=1)
        current = jnp.einsum(
            "pkrs,pksc->prc",
            blocks[:, layer_index],
            selected_rows,
            preferred_element_type=jnp.float32,
        )
    contrast_rows = jnp.take(contrast_lookup, sample_index, axis=0)
    current = current * contrast_rows[:, :, None]
    for layer_index in reversed(range(blocks.shape[1])):
        rounded = current.astype(jnp.bfloat16)
        summand_terms = jnp.einsum(
            "pkrs,prc->pksc", blocks[:, layer_index], rounded, preferred_element_type=jnp.float32
        )
        owner_row = owners[:, layer_index, :]
        positioned_rows = jnp.take_along_axis(summand_terms, owner_row[:, :, None, None], axis=1)
        if layer_index == 0:
            current = jnp.sum(positioned_rows, axis=0)
        else:
            first_bit, second_bit = section_bits(layer_index, digit_count)
            current = spread(jnp.swapaxes(positioned_rows, 0, 1), first_bit, second_bit)
    return current


def solution(mesh):
    return jax.shard_map(
        per_device,
        mesh=mesh,
        in_specs=(
            P(("groups", "box"), None, None),
            P(("groups", "box"), None, None, None, None),
            P(("groups", "box")),
            P("box", None),
            P("box", None, None),
        ),
        out_specs=P(("groups", "box"), None, None),
        check_vma=False,
    )
```

profile of v0, /device:TPU:0, one launch (start us, length us, event | category | flops | bytes accessed | tf_op | source)
XLA Modules:
  0.0 552.1 jit_solution(16012756968478527235)
XLA Ops:
  10.6 3.6 fusion.56
  21.2 34.5 %collective-permute-done.1 = bf16[2,4,256,384]{2,3,1,0:T(8,128)(2,1)S(1)} collective-permute-done((bf16[2,4,256,384]{2,3,1,0:T(8,128)(2,1)S(1)}, bf16[2,4,256,384]{2,3,1,0:T(8,128)(2,1)S(1)}, u32[]{:S(2)}, u32[]{:S(2)}) %collective-permute-start.1) | collective-permute-done | bytes 1572896 | tf_op jit(solution)/shard_map/ppermute | solution.py:8
  56.8 3.3 maximum_select_fusion
  62.6 3.6 fusion.61
  68.0 17.2 %collective-permute-done.2 = bf16[4,256,384]{1,2,0:T(8,128)(2,1)S(1)} collective-permute-done((bf16[4,256,384]{1,2,0:T(8,128)(2,1)S(1)}, bf16[4,256,384]{1,2,0:T(8,128)(2,1)S(1)}, u32[]{:S(2)}, u32[]{:S(2)}) %collective-permute-start.2) | collective-permute-done | bytes 786464 | tf_op jit(solution)/shard_map/ppermute | solution.py:8
  89.4 66.9 %collective-permute-done.3 = bf16[2,4,256,384]{2,3,1,0:T(8,128)(2,1)S(1)} collective-permute-done((bf16[2,4,256,384]{2,3,1,0:T(8,128)(2,1)S(1)}, bf16[2,4,256,384]{2,3,1,0:T(8,128)(2,1)S(1)}, u32[]{:S(2)}, u32[]{:S(2)}) %collective-permute-start.3) | collective-permute-done | bytes 1572896 | tf_op jit(solution)/shard_map/ppermute | solution.py:8
  157.4 3.3 maximum_select_fusion.1
  163.2 3.6 fusion.66
  172.2 49.2 %all-gather = f32[16,1,256]{2,1,0:T(1,128)S(1)} all-gather(f32[1,1,256]{2,1,0:T(1,128)S(1)} %bitcast.346), channel_id=1, replica_groups=mesh['groups'=2,'box'=16] {'box'}, dimensions={0}, use_global_device_ids=true | all-gather | bytes 17408 | tf_op jit(solution)/shard_map/all_gather | solution.py:47
  221.4 6.1 %gather_fusion = f32[1024]{0:T(1024)S(1)} fusion(f32[4096]{0:T(1024)S(1)} %bitcast.311, s32[1024]{0:T(1024)S(1)} %broadcast_clamp_fusion), kind=kCustom, calls=%fused_computation.8 | custom fusion | bytes 12288 | tf_op jit(solution)/shard_map/jit(_take)/gather | solution.py:72
  228.8 3.3 maximum_select_fusion.2
  234.6 7.7 %convolution_bitcast_fusion.3 = f32[4,4,256,384]{2,3,1,0:T(8,128)} fusion(bf16[4,4,4,256,256]{4,3,2,1,0:T(8,128)(2,1)} %param.10, bf16[4,4,256,384]{2,3,1,0:T(8,128)(2,1)} %bitcast.327, pred[4,4]{1,0:T(4,128)(4,1)S(1)} %and_bitcast_fusion.4, f32[4,256]{1,0:T(4,128)S(1)} %and_select_fusion), kind=kOutput, calls=%fused_computation.42 | convolution fusion | flops 1612972032 | bytes 13635600 | tf_op jit(solution)/shard_map/pkrs,prc->pksc/dot_general | solution.py:76
  242.3 6.4 %gather_fusion.5 = f32[16,256,384]{1,2,0:T(8,128)} fusion(f32[4,4,256,384]{2,3,1,0:T(8,128)} %convolution_bitcast_fusion.3, s32[16]{0:T(128)S(1)} %reshape.226), kind=kCustom, calls=%fused_computation.1.clone | custom fusion | bytes 12583040 | tf_op jit(solution)/shard_map/jit(take_along_axis)/gather | solution.py:80
  248.6 6.6 %copy.65 = f32[4,4,256,384]{3,2,0,1:T(8,128)} copy(f32[4,4,256,384]{2,3,1,0:T(8,128)} %bitcast.319) | data formatting | bytes 12582912 | tf_op jit(solution)/shard_map/jit(take_along_axis)/gather | solution.py:80
  255.2 3.6 broadcast_select_fusion.2
  259.5 5.3 collective-permute-done.6
  266.8 36.7 %collective-permute-done.7 = f32[4,256,384]{2,1,0:T(8,128)} collective-permute-done((f32[4,256,384]{2,1,0:T(8,128)}, f32[4,256,384]{2,1,0:T(8,128)}, u32[]{:S(2)}, u32[]{:S(2)}) %collective-permute-start.7) | collective-permute-done | bytes 1572896 | tf_op jit(solution)/shard_map/ppermute | solution.py:8
  303.6 5.8 %convolution_bitcast_fusion.2 = f32[4,4,256,384]{2,3,1,0:T(8,128)} fusion(bf16[4,4,4,256,256]{4,3,2,1,0:T(8,128)(2,1)} %param.10, f32[4,256,384]{2,1,0:T(8,128)} %collective-permute-done.7, f32[2,4,256,384]{3,2,1,0:T(8,128)S(1)} %fusion.3, pred[]{:T(512)S(6)} %eq.40), kind=kOutput, calls=%fused_computation.41 | convolution fusion | flops 806486016 | bytes 13107201 | tf_op jit(solution)/shard_map/pkrs,prc->pksc/dot_general | solution.py:76
  309.3 6.4 %gather_fusion.6 = f32[16,256,384]{1,2,0:T(8,128)} fusion(f32[4,4,256,384]{2,3,1,0:T(8,128)} %convolution_bitcast_fusion.2, s32[16]{0:T(128)S(1)} %reshape.231), kind=kCustom, calls=%fused_computation.5.clone | custom fusion | bytes 12583040 | tf_op jit(solution)/shard_map/jit(take_along_axis)/gather | solution.py:80
  315.7 6.6 %copy.71 = f32[4,4,256,384]{3,2,0,1:T(8,128)} copy(f32[4,4,256,384]{2,3,1,0:T(8,128)} %bitcast.320) | data formatting | bytes 12582912 | tf_op jit(solution)/shard_map/jit(take_along_axis)/gather | solution.py:80
  322.3 3.6 broadcast_select_fusion.1
  326.3 69.5 %collective-permute-done.8 = f32[2,4,256,384]{3,2,1,0:T(8,128)S(1)} collective-permute-done((f32[2,4,256,384]{3,2,1,0:T(8,128)S(1)}, f32[2,4,256,384]{3,2,1,0:T(8,128)S(1)}, u32[]{:S(2)}, u32[]{:S(2)}) %collective-permute-start.8) | collective-permute-done | bytes 3145760 | tf_op jit(solution)/shard_map/ppermute | solution.py:8
  397.7 69.6 %collective-permute-done.9 = f32[4,256,384]{2,1,0:T(8,128)} collective-permute-done((f32[4,256,384]{2,1,0:T(8,128)}, f32[4,256,384]{2,1,0:T(8,128)}, u32[]{:S(2)}, u32[]{:S(2)}) %collective-permute-start.9) | collective-permute-done | bytes 1572896 | tf_op jit(solution)/shard_map/ppermute | solution.py:8
  467.4 5.8 %convolution_bitcast_fusion.1 = f32[4,4,256,384]{2,3,1,0:T(8,128)} fusion(bf16[4,4,4,256,256]{4,3,2,1,0:T(8,128)(2,1)} %param.10, f32[4,256,384]{2,1,0:T(8,128)} %collective-permute-done.9, f32[2,4,256,384]{3,2,1,0:T(8,128)S(1)} %fusion.1, pred[]{:T(512)S(6)} %eq.42), kind=kOutput, calls=%fused_computation.40 | convolution fusion | flops 806486016 | bytes 13107201 | tf_op jit(solution)/shard_map/pkrs,prc->pksc/dot_general | solution.py:76
  473.1 6.4 %gather_fusion.7 = f32[16,256,384]{1,2,0:T(8,128)} fusion(f32[4,4,256,384]{2,3,1,0:T(8,128)} %convolution_bitcast_fusion.1, s32[16]{0:T(128)S(1)} %reshape.236), kind=kCustom, calls=%fused_computation.6.clone | custom fusion | bytes 12583040 | tf_op jit(solution)/shard_map/jit(take_along_axis)/gather | solution.py:80
  479.5 6.6 %copy.77 = f32[4,4,256,384]{3,2,0,1:T(8,128)} copy(f32[4,4,256,384]{2,3,1,0:T(8,128)} %bitcast.321) | data formatting | bytes 12582912 | tf_op jit(solution)/shard_map/jit(take_along_axis)/gather | solution.py:80
  486.1 3.6 broadcast_select_fusion
  490.7 5.6 %collective-permute-done.10 = f32[2,4,256,384]{3,2,1,0:T(8,128)S(1)} collective-permute-done((f32[2,4,256,384]{3,2,1,0:T(8,128)S(1)}, f32[2,4,256,384]{3,2,1,0:T(8,128)S(1)}, u32[]{:S(2)}, u32[]{:S(2)}) %collective-permute-start.10) | collective-permute-done | bytes 3145760 | tf_op jit(solution)/shard_map/ppermute | solution.py:8
  499.0 35.8 %collective-permute-done.11 = f32[4,256,384]{2,1,0:T(8,128)} collective-permute-done((f32[4,256,384]{2,1,0:T(8,128)}, f32[4,256,384]{2,1,0:T(8,128)}, u32[]{:S(2)}, u32[]{:S(2)}) %collective-permute-start.11) | collective-permute-done | bytes 1572896 | tf_op jit(solution)/shard_map/ppermute | solution.py:8
  534.8 5.8 %convolution_bitcast_fusion = f32[4,4,256,384]{2,3,1,0:T(8,128)} fusion(bf16[4,4,4,256,256]{4,3,2,1,0:T(8,128)(2,1)} %param.10, f32[4,256,384]{2,1,0:T(8,128)} %collective-permute-done.11, f32[2,4,256,384]{3,2,1,0:T(8,128)S(1)} %bitcast_add_fusion, pred[]{:T(512)S(6)} %eq.40), kind=kOutput, calls=%fused_computation.39 | convolution fusion | flops 806486016 | bytes 13107201 | tf_op jit(solution)/shard_map/pkrs,prc->pksc/dot_general | solution.py:76
  540.6 6.4 %gather_fusion.8 = f32[16,256,384]{1,2,0:T(8,128)} fusion(f32[4,4,256,384]{2,3,1,0:T(8,128)} %convolution_bitcast_fusion, s32[16]{0:T(128)S(1)} %reshape.241), kind=kCustom, calls=%fused_computation.7.clone | custom fusion | bytes 12583040 | tf_op jit(solution)/shard_map/jit(take_along_axis)/gather | solution.py:80
  547.0 3.5 select_reduce_fusion
  (86 shorter events, 50.0 us)
Async XLA Ops:
  14.2 2.5 collective-permute-start
  18.1 37.6 %collective-permute-start.1 = (bf16[2,4,256,384]{2,3,1,0:T(8,128)(2,1)S(1)}, bf16[2,4,256,384]{2,3,1,0:T(8,128)(2,1)S(1)}, u32[]{:S(2)}, u32[]{:S(2)}) collective-permute-start(bf16[2,4,256,384]{2,3,1,0:T(8,128)(2,1)S(1)} %get-tuple-element.16), channel_id=1, source_target_pairs={{0,2},{1,3},{2,0},{3,1},{4,6},{5,7},{6,4},{7,5},{8,10},{9,11},{10,... | collective-permute-start | bytes 4718600 | tf_op jit(solution)/shard_map/ppermute | solution.py:8
  55.7 1.1 copy-start.2
  66.1 19.1 %collective-permute-start.2 = (bf16[4,256,384]{1,2,0:T(8,128)(2,1)S(1)}, bf16[4,256,384]{1,2,0:T(8,128)(2,1)S(1)}, u32[]{:S(2)}, u32[]{:S(2)}) collective-permute-start(bf16[4,256,384]{1,2,0:T(8,128)(2,1)S(1)} %fusion.61), channel_id=1, source_target_pairs={{0,4},{1,5},{2,6},{3,7},{4,0},{5,1},{6,2},{7,3},{8,12},{9,13},{10,... | collective-permute-start | bytes 2359304 | tf_op jit(solution)/shard_map/ppermute | solution.py:8
  86.7 69.6 %collective-permute-start.3 = (bf16[2,4,256,384]{2,3,1,0:T(8,128)(2,1)S(1)}, bf16[2,4,256,384]{2,3,1,0:T(8,128)(2,1)S(1)}, u32[]{:S(2)}, u32[]{:S(2)}) collective-permute-start(bf16[2,4,256,384]{2,3,1,0:T(8,128)(2,1)S(1)} %get-tuple-element.12), channel_id=1, source_target_pairs={{0,8},{1,9},{2,10},{3,11},{4,12},{5,13},{6,14},{7,15},{8,0},{9,1},... | collective-permute-start | bytes 4718600 | tf_op jit(solution)/shard_map/ppermute | solution.py:8
  156.3 1.1 copy-start.1
  166.7 2.4 collective-permute-start.4
  169.2 2.6 copy-start.3
  169.2 3.0 copy-start.4
  170.6 57.0 %collective-permute-start.5 = (bf16[2,4,256,384]{2,3,1,0:T(8,128)(2,1)S(1)}, bf16[2,4,256,384]{2,3,1,0:T(8,128)(2,1)S(1)}, u32[]{:S(2)}, u32[]{:S(2)}) collective-permute-start(bf16[2,4,256,384]{2,3,1,0:T(8,128)(2,1)S(1)} %get-tuple-element.8), channel_id=1, source_target_pairs={{0,2},{1,3},{2,0},{3,1},{4,6},{5,7},{6,4},{7,5},{8,10},{9,11},{10,... | collective-permute-start | bytes 4718600 | tf_op jit(solution)/shard_map/ppermute | solution.py:8
  227.6 1.1 copy-start
  259.1 5.7 %collective-permute-start.6 = (f32[2,4,256,384]{3,2,1,0:T(8,128)S(1)}, f32[2,4,256,384]{3,2,1,0:T(8,128)S(1)}, u32[]{:S(2)}, u32[]{:S(2)}) collective-permute-start(f32[2,4,256,384]{3,2,1,0:T(8,128)S(1)} %select_bitcast_fusion.2), channel_id=1, source_target_pairs={{0,1},{1,0},{2,3},{3,2},{4,5},{5,4},{6,7},{7,6},{8,9},{9,8},{10,11... | collective-permute-start | bytes 9437192 | tf_op jit(solution)/shard_map/ppermute | solution.py:8
  266.6 37.0 %collective-permute-start.7 = (f32[4,256,384]{2,1,0:T(8,128)}, f32[4,256,384]{2,1,0:T(8,128)}, u32[]{:S(2)}, u32[]{:S(2)}) collective-permute-start(f32[4,256,384]{2,1,0:T(8,128)} %select_bitcast_fusion.5), channel_id=1, source_target_pairs={{0,2},{1,3},{2,0},{3,1},{4,6},{5,7},{6,4},{7,5},{8,10},{9,11},{10,... | collective-permute-start | bytes 4718600 | tf_op jit(solution)/shard_map/ppermute | solution.py:8
  326.2 69.6 %collective-permute-start.8 = (f32[2,4,256,384]{3,2,1,0:T(8,128)S(1)}, f32[2,4,256,384]{3,2,1,0:T(8,128)S(1)}, u32[]{:S(2)}, u32[]{:S(2)}) collective-permute-start(f32[2,4,256,384]{3,2,1,0:T(8,128)S(1)} %select_bitcast_fusion.1), channel_id=1, source_target_pairs={{0,4},{1,5},{2,6},{3,7},{4,0},{5,1},{6,2},{7,3},{8,12},{9,13},{10,... | collective-permute-start | bytes 9437192 | tf_op jit(solution)/shard_map/ppermute | solution.py:8
  397.5 69.8 %collective-permute-start.9 = (f32[4,256,384]{2,1,0:T(8,128)}, f32[4,256,384]{2,1,0:T(8,128)}, u32[]{:S(2)}, u32[]{:S(2)}) collective-permute-start(f32[4,256,384]{2,1,0:T(8,128)} %select_bitcast_fusion.4), channel_id=1, source_target_pairs={{0,8},{1,9},{2,10},{3,11},{4,12},{5,13},{6,14},{7,15},{8,0},{9,1},... | collective-permute-start | bytes 4718600 | tf_op jit(solution)/shard_map/ppermute | solution.py:8
  490.6 5.7 %collective-permute-start.10 = (f32[2,4,256,384]{3,2,1,0:T(8,128)S(1)}, f32[2,4,256,384]{3,2,1,0:T(8,128)S(1)}, u32[]{:S(2)}, u32[]{:S(2)}) collective-permute-start(f32[2,4,256,384]{3,2,1,0:T(8,128)S(1)} %select_bitcast_fusion), channel_id=1, source_target_pairs={{0,1},{1,0},{2,3},{3,2},{4,5},{5,4},{6,7},{7,6},{8,9},{9,8},{10,11... | collective-permute-start | bytes 9437192 | tf_op jit(solution)/shard_map/ppermute | solution.py:8
  498.1 36.8 %collective-permute-start.11 = (f32[4,256,384]{2,1,0:T(8,128)}, f32[4,256,384]{2,1,0:T(8,128)}, u32[]{:S(2)}, u32[]{:S(2)}) collective-permute-start(f32[4,256,384]{2,1,0:T(8,128)} %select_bitcast_fusion.3), channel_id=1, source_target_pairs={{0,2},{1,3},{2,0},{3,1},{4,6},{5,7},{6,4},{7,5},{8,10},{9,11},{10,... | collective-permute-start | bytes 4718600 | tf_op jit(solution)/shard_map/ppermute | solution.py:8
where the time goes:
time: 553 us; the launch traced here: 552 us
  waiting for transfers between devices  345 us (62%)
  local copies, waits for them, and re-layouts  74.2 us (13%)
  blocking collectives  49.2 us (9%)
  other arithmetic  36.8 us (7%)
  matrix products  35.7 us (6%)
  starting transfers between devices  10.5 us (2%)
    ppermute x12, waiting for transfers between devices, partner(): lax.ppermute(x, axis, [(i, i ^ 1 << distance) for i in range(lax.axis_siz...  345 us
    all_gather x1, blocking collectives, per_device(): contrast_lookup = lax.all_gather(contrast, 'box', axis=0, tiled=True)  49.2 us
    gather x11, local copies, waits for them, and re-layouts, per_device(): jnp.take_along_axis(summand_terms, owner_row[:, :, None, None], axis=1)  45.6 us
    dot_general x4, matrix products, per_device(): jnp.einsum('pkrs,prc->pksc', blocks[:, layer_index], rounded, preferred_e...  25 us
    gather x9, local copies, waits for them, and re-layouts, per_device(): jnp.take_along_axis(gathered_groups, inverse[:, :, None, None], axis=1)  13.6 us
  transfers between devices with their start and end apart: 12, of which 11 were waited for; matrix products, arithmetic and copies ran while one was open for 1% of the time, Pallas kernels for 0%

commit v1 on v0

--- a/solution.py
+++ b/solution.py
@@ -44,7 +44,9 @@
 
 
 def per_device(right_sides, blocks, contrast, sample_index, owners):
-    contrast_lookup = lax.all_gather(contrast, "box", axis=0, tiled=True)
+    contrast_lookup = jnp.concatenate(
+        lax.all_to_all(jnp.stack([contrast] * lax.axis_size("box")), "box", 0, 0), axis=0
+    )
     digit_count = (lax.axis_size("box").bit_length() - 1) // 2
     resident_boxes = right_sides.shape[0]
     slots = jnp.arange(4, dtype=jnp.int32)

time: 553 us -> 536 us (0.969)
  blocking collectives: 49.2 us -> 0 us
  waiting for transfers between devices: 345 us -> 365 us
  starting transfers between devices: 10.5 us -> 22.7 us
    all_gather x1 -> x0, blocking collectives: 49.2 us -> none  [per_device(): contrast_lookup = lax.all_gather(contrast, 'box', axis=0, tiled=True)]
    ppermute x12, waiting for transfers between devices: 345 us -> 362 us  [partner(): lax.ppermute(x, axis, [(i, i ^ 1 << distance) for i in range(lax.axis_siz...]
    ppermute x12, starting transfers between devices: 10.5 us -> 17.2 us  [partner(): lax.ppermute(x, axis, [(i, i ^ 1 << distance) for i in range(lax.axis_siz...]
    all_to_all x0 -> x1, starting transfers between devices: none -> 5.59 us  [per_device(): lax.all_to_all(jnp.stack([contrast] * lax.axis_size('box')), 'box', 0, 0)]
  transfers between devices with their start and end apart: 12 -> 13, of which waited for: 11 -> 12; matrix products, arithmetic and copies ran while one was open for 1% -> 2% of each run, Pallas kernels for 0% -> 0%
where the time goes in v1:
time: 536 us; the launch traced here: 535 us
  waiting for transfers between devices  365 us (68%)
  local copies, waits for them, and re-layouts  74.9 us (14%)
  other arithmetic  36.9 us (7%)
  matrix products  35.7 us (7%)
  starting transfers between devices  22.7 us (4%)
    ppermute x12, waiting for transfers between devices, partner(): lax.ppermute(x, axis, [(i, i ^ 1 << distance) for i in range(lax.axis_siz...  362 us
    gather x11, local copies, waits for them, and re-layouts, per_device(): jnp.take_along_axis(summand_terms, owner_row[:, :, None, None], axis=1)  45.6 us
    dot_general x4, matrix products, per_device(): jnp.einsum('pkrs,prc->pksc', blocks[:, layer_index], rounded, preferred_e...  25 us
    ppermute x12, starting transfers between devices, partner(): lax.ppermute(x, axis, [(i, i ^ 1 << distance) for i in range(lax.axis_siz...  17.2 us
    gather x9, local copies, waits for them, and re-layouts, per_device(): jnp.take_along_axis(gathered_groups, inverse[:, :, None, None], axis=1)  13.6 us
  transfers between devices with their start and end apart: 13, of which 12 were waited for; matrix products, arithmetic and copies ran while one was open for 2% of the time, Pallas kernels for 0%

profile of v1, /device:TPU:0, one launch (start us, length us, event | category | flops | bytes accessed | tf_op | source)
XLA Modules:
  0.0 535.4 jit_solution(12141529278424429905)
XLA Ops:
  10.6 3.6 fusion.56
  21.2 34.5 %collective-permute-done.1 = bf16[2,4,256,384]{2,3,1,0:T(8,128)(2,1)S(1)} collective-permute-done((bf16[2,4,256,384]{2,3,1,0:T(8,128)(2,1)S(1)}, bf16[2,4,256,384]{2,3,1,0:T(8,128)(2,1)S(1)}, u32[]{:S(2)}, u32[]{:S(2)}) %collective-permute-start.1) | collective-permute-done | bytes 1572896 | tf_op jit(solution)/shard_map/ppermute | solution.py:8
  56.8 3.4 maximum_select_fusion
  62.6 3.6 fusion.61
  68.1 17.2 %collective-permute-done.2 = bf16[4,256,384]{1,2,0:T(8,128)(2,1)S(1)} collective-permute-done((bf16[4,256,384]{1,2,0:T(8,128)(2,1)S(1)}, bf16[4,256,384]{1,2,0:T(8,128)(2,1)S(1)}, u32[]{:S(2)}, u32[]{:S(2)}) %collective-permute-start.2) | collective-permute-done | bytes 786464 | tf_op jit(solution)/shard_map/ppermute | solution.py:8
  89.4 66.9 %collective-permute-done.3 = bf16[2,4,256,384]{2,3,1,0:T(8,128)(2,1)S(1)} collective-permute-done((bf16[2,4,256,384]{2,3,1,0:T(8,128)(2,1)S(1)}, bf16[2,4,256,384]{2,3,1,0:T(8,128)(2,1)S(1)}, u32[]{:S(2)}, u32[]{:S(2)}) %collective-permute-start.3) | collective-permute-done | bytes 1572896 | tf_op jit(solution)/shard_map/ppermute | solution.py:8
  157.5 3.4 maximum_select_fusion.1
  163.3 3.6 fusion.66
  167.5 5.6 %all-to-all-start = ((f32[16,1,256]{2,1,0:T(1,128)}), f32[16,1,256]{2,1,0:T(1,128)S(1)}, u32[]{:S(2)}, u32[]{:S(2)}) async-start(f32[16,1,256]{2,1,0:T(1,128)} %stack.109), calls=%async_computation | async-start | bytes 32768 | tf_op jit(solution)/shard_map/all_to_all | solution.py:48
  179.7 6.1 %gather_fusion = f32[1024]{0:T(1024)S(1)} fusion(f32[4096]{0:T(1024)S(1)} %bitcast.310, s32[1024]{0:T(1024)S(1)} %broadcast_clamp_fusion), kind=kCustom, calls=%fused_computation.8 | custom fusion | bytes 12288 | tf_op jit(solution)/shard_map/jit(_take)/gather | solution.py:74
  185.9 25.6 %collective-permute-done.5 = bf16[2,4,256,384]{2,3,1,0:T(8,128)(2,1)S(1)} collective-permute-done((bf16[2,4,256,384]{2,3,1,0:T(8,128)(2,1)S(1)}, bf16[2,4,256,384]{2,3,1,0:T(8,128)(2,1)S(1)}, u32[]{:S(2)}, u32[]{:S(2)}) %collective-permute-start.5) | collective-permute-done | bytes 1572896 | tf_op jit(solution)/shard_map/ppermute | solution.py:8
  218.4 7.7 %convolution_bitcast_fusion.3 = f32[4,4,256,384]{2,3,1,0:T(8,128)} fusion(bf16[4,4,4,256,256]{4,3,2,1,0:T(8,128)(2,1)} %param.10, bf16[4,4,256,384]{2,3,1,0:T(8,128)(2,1)} %bitcast.326, pred[4,4]{1,0:T(4,128)(4,1)S(1)} %and_bitcast_fusion.4, f32[4,256]{1,0:T(4,128)S(1)} %and_select_fusion), kind=kOutput, calls=%fused_computation.42 | convolution fusion | flops 1612972032 | bytes 13635600 | tf_op jit(solution)/shard_map/pkrs,prc->pksc/dot_general | solution.py:78
  226.1 6.4 %gather_fusion.5 = f32[16,256,384]{1,2,0:T(8,128)} fusion(f32[4,4,256,384]{2,3,1,0:T(8,128)} %convolution_bitcast_fusion.3, s32[16]{0:T(128)S(1)} %reshape.236), kind=kCustom, calls=%fused_computation.1.clone | custom fusion | bytes 12583040 | tf_op jit(solution)/shard_map/jit(take_along_axis)/gather | solution.py:82
  232.5 6.6 %copy.65 = f32[4,4,256,384]{3,2,0,1:T(8,128)} copy(f32[4,4,256,384]{2,3,1,0:T(8,128)} %bitcast.318) | data formatting | bytes 12582912 | tf_op jit(solution)/shard_map/jit(take_along_axis)/gather | solution.py:82
  239.1 3.6 broadcast_select_fusion.2
  243.1 5.6 %collective-permute-done.6 = f32[2,4,256,384]{3,2,1,0:T(8,128)S(1)} collective-permute-done((f32[2,4,256,384]{3,2,1,0:T(8,128)S(1)}, f32[2,4,256,384]{3,2,1,0:T(8,128)S(1)}, u32[]{:S(2)}, u32[]{:S(2)}) %collective-permute-start.6) | collective-permute-done | bytes 3145760 | tf_op jit(solution)/shard_map/ppermute | solution.py:8
  252.2 35.0 %collective-permute-done.7 = f32[4,256,384]{2,1,0:T(8,128)} collective-permute-done((f32[4,256,384]{2,1,0:T(8,128)}, f32[4,256,384]{2,1,0:T(8,128)}, u32[]{:S(2)}, u32[]{:S(2)}) %collective-permute-start.7) | collective-permute-done | bytes 1572896 | tf_op jit(solution)/shard_map/ppermute | solution.py:8
  287.2 5.8 %convolution_bitcast_fusion.2 = f32[4,4,256,384]{2,3,1,0:T(8,128)} fusion(bf16[4,4,4,256,256]{4,3,2,1,0:T(8,128)(2,1)} %param.10, f32[4,256,384]{2,1,0:T(8,128)} %collective-permute-done.7, f32[2,4,256,384]{3,2,1,0:T(8,128)S(1)} %fusion.3, pred[]{:T(512)S(6)} %eq.40), kind=kOutput, calls=%fused_computation.41 | convolution fusion | flops 806486016 | bytes 13107201 | tf_op jit(solution)/shard_map/pkrs,prc->pksc/dot_general | solution.py:78
  293.0 6.4 %gather_fusion.6 = f32[16,256,384]{1,2,0:T(8,128)} fusion(f32[4,4,256,384]{2,3,1,0:T(8,128)} %convolution_bitcast_fusion.2, s32[16]{0:T(128)S(1)} %reshape.241), kind=kCustom, calls=%fused_computation.5.clone | custom fusion | bytes 12583040 | tf_op jit(solution)/shard_map/jit(take_along_axis)/gather | solution.py:82
  299.4 6.6 %copy.71 = f32[4,4,256,384]{3,2,0,1:T(8,128)} copy(f32[4,4,256,384]{2,3,1,0:T(8,128)} %bitcast.319) | data formatting | bytes 12582912 | tf_op jit(solution)/shard_map/jit(take_along_axis)/gather | solution.py:82
  306.0 3.6 broadcast_select_fusion.1
  311.5 67.7 %collective-permute-done.8 = f32[2,4,256,384]{3,2,1,0:T(8,128)S(1)} collective-permute-done((f32[2,4,256,384]{3,2,1,0:T(8,128)S(1)}, f32[2,4,256,384]{3,2,1,0:T(8,128)S(1)}, u32[]{:S(2)}, u32[]{:S(2)}) %collective-permute-start.8) | collective-permute-done | bytes 3145760 | tf_op jit(solution)/shard_map/ppermute | solution.py:8
  383.6 67.0 %collective-permute-done.9 = f32[4,256,384]{2,1,0:T(8,128)} collective-permute-done((f32[4,256,384]{2,1,0:T(8,128)}, f32[4,256,384]{2,1,0:T(8,128)}, u32[]{:S(2)}, u32[]{:S(2)}) %collective-permute-start.9) | collective-permute-done | bytes 1572896 | tf_op jit(solution)/shard_map/ppermute | solution.py:8
  450.6 5.8 %convolution_bitcast_fusion.1 = f32[4,4,256,384]{2,3,1,0:T(8,128)} fusion(bf16[4,4,4,256,256]{4,3,2,1,0:T(8,128)(2,1)} %param.10, f32[4,256,384]{2,1,0:T(8,128)} %collective-permute-done.9, f32[2,4,256,384]{3,2,1,0:T(8,128)S(1)} %fusion.1, pred[]{:T(512)S(6)} %eq.42), kind=kOutput, calls=%fused_computation.40 | convolution fusion | flops 806486016 | bytes 13107201 | tf_op jit(solution)/shard_map/pkrs,prc->pksc/dot_general | solution.py:78
  456.4 6.4 %gather_fusion.7 = f32[16,256,384]{1,2,0:T(8,128)} fusion(f32[4,4,256,384]{2,3,1,0:T(8,128)} %convolution_bitcast_fusion.1, s32[16]{0:T(128)S(1)} %reshape.246), kind=kCustom, calls=%fused_computation.6.clone | custom fusion | bytes 12583040 | tf_op jit(solution)/shard_map/jit(take_along_axis)/gather | solution.py:82
  462.8 6.6 %copy.77 = f32[4,4,256,384]{3,2,0,1:T(8,128)} copy(f32[4,4,256,384]{2,3,1,0:T(8,128)} %bitcast.320) | data formatting | bytes 12582912 | tf_op jit(solution)/shard_map/jit(take_along_axis)/gather | solution.py:82
  469.3 3.6 broadcast_select_fusion
  473.9 5.6 %collective-permute-done.10 = f32[2,4,256,384]{3,2,1,0:T(8,128)S(1)} collective-permute-done((f32[2,4,256,384]{3,2,1,0:T(8,128)S(1)}, f32[2,4,256,384]{3,2,1,0:T(8,128)S(1)}, u32[]{:S(2)}, u32[]{:S(2)}) %collective-permute-start.10) | collective-permute-done | bytes 3145760 | tf_op jit(solution)/shard_map/ppermute | solution.py:8
  483.0 35.1 %collective-permute-done.11 = f32[4,256,384]{2,1,0:T(8,128)} collective-permute-done((f32[4,256,384]{2,1,0:T(8,128)}, f32[4,256,384]{2,1,0:T(8,128)}, u32[]{:S(2)}, u32[]{:S(2)}) %collective-permute-start.11) | collective-permute-done | bytes 1572896 | tf_op jit(solution)/shard_map/ppermute | solution.py:8
  518.0 5.8 %convolution_bitcast_fusion = f32[4,4,256,384]{2,3,1,0:T(8,128)} fusion(bf16[4,4,4,256,256]{4,3,2,1,0:T(8,128)(2,1)} %param.10, f32[4,256,384]{2,1,0:T(8,128)} %collective-permute-done.11, f32[2,4,256,384]{3,2,1,0:T(8,128)S(1)} %bitcast_add_fusion, pred[]{:T(512)S(6)} %eq.40), kind=kOutput, calls=%fused_computation.39 | convolution fusion | flops 806486016 | bytes 13107201 | tf_op jit(solution)/shard_map/pkrs,prc->pksc/dot_general | solution.py:78
  523.8 6.4 %gather_fusion.8 = f32[16,256,384]{1,2,0:T(8,128)} fusion(f32[4,4,256,384]{2,3,1,0:T(8,128)} %convolution_bitcast_fusion, s32[16]{0:T(128)S(1)} %reshape.251), kind=kCustom, calls=%fused_computation.7.clone | custom fusion | bytes 12583040 | tf_op jit(solution)/shard_map/jit(take_along_axis)/gather | solution.py:82
  530.2 3.5 select_reduce_fusion
  (88 shorter events, 61.1 us)
Async XLA Ops:
  14.2 2.5 collective-permute-start
  18.1 37.6 %collective-permute-start.1 = (bf16[2,4,256,384]{2,3,1,0:T(8,128)(2,1)S(1)}, bf16[2,4,256,384]{2,3,1,0:T(8,128)(2,1)S(1)}, u32[]{:S(2)}, u32[]{:S(2)}) collective-permute-start(bf16[2,4,256,384]{2,3,1,0:T(8,128)(2,1)S(1)} %get-tuple-element.16), channel_id=1, source_target_pairs={{0,2},{1,3},{2,0},{3,1},{4,6},{5,7},{6,4},{7,5},{8,10},{9,11},{10,... | collective-permute-start | bytes 4718600 | tf_op jit(solution)/shard_map/ppermute | solution.py:8
  55.7 1.2 copy-start.2
  66.2 19.1 %collective-permute-start.2 = (bf16[4,256,384]{1,2,0:T(8,128)(2,1)S(1)}, bf16[4,256,384]{1,2,0:T(8,128)(2,1)S(1)}, u32[]{:S(2)}, u32[]{:S(2)}) collective-permute-start(bf16[4,256,384]{1,2,0:T(8,128)(2,1)S(1)} %fusion.61), channel_id=1, source_target_pairs={{0,4},{1,5},{2,6},{3,7},{4,0},{5,1},{6,2},{7,3},{8,12},{9,13},{10,... | collective-permute-start | bytes 2359304 | tf_op jit(solution)/shard_map/ppermute | solution.py:8
  86.7 69.6 %collective-permute-start.3 = (bf16[2,4,256,384]{2,3,1,0:T(8,128)(2,1)S(1)}, bf16[2,4,256,384]{2,3,1,0:T(8,128)(2,1)S(1)}, u32[]{:S(2)}, u32[]{:S(2)}) collective-permute-start(bf16[2,4,256,384]{2,3,1,0:T(8,128)(2,1)S(1)} %get-tuple-element.12), channel_id=1, source_target_pairs={{0,8},{1,9},{2,10},{3,11},{4,12},{5,13},{6,14},{7,15},{8,0},{9,1},... | collective-permute-start | bytes 4718600 | tf_op jit(solution)/shard_map/ppermute | solution.py:8
  156.3 1.2 copy-start.1
  163.3 3.7 copy-start.4
  166.8 6.3 %collective-permute-start.4 = (bf16[4,256,384]{1,2,0:T(8,128)(2,1)S(1)}, bf16[4,256,384]{1,2,0:T(8,128)(2,1)S(1)}, u32[]{:S(2)}, u32[]{:S(2)}) collective-permute-start(bf16[4,256,384]{1,2,0:T(8,128)(2,1)S(1)} %fusion.66), channel_id=1, source_target_pairs={{0,1},{1,0},{2,3},{3,2},{4,5},{5,4},{6,7},{7,6},{8,9},{9,8},{10,11... | collective-permute-start | bytes 2359304 | tf_op jit(solution)/shard_map/ppermute | solution.py:8
  167.5 12.1 %all-to-all-start = ((f32[16,1,256]{2,1,0:T(1,128)}), f32[16,1,256]{2,1,0:T(1,128)S(1)}, u32[]{:S(2)}, u32[]{:S(2)}) async-start(f32[16,1,256]{2,1,0:T(1,128)} %stack.109), calls=%async_computation | async-start | bytes 32768 | tf_op jit(solution)/shard_map/all_to_all | solution.py:48
  173.3 3.3 copy-start.3
  174.6 36.8 %collective-permute-start.5 = (bf16[2,4,256,384]{2,3,1,0:T(8,128)(2,1)S(1)}, bf16[2,4,256,384]{2,3,1,0:T(8,128)(2,1)S(1)}, u32[]{:S(2)}, u32[]{:S(2)}) collective-permute-start(bf16[2,4,256,384]{2,3,1,0:T(8,128)(2,1)S(1)} %get-tuple-element.8), channel_id=1, source_target_pairs={{0,2},{1,3},{2,0},{3,1},{4,6},{5,7},{6,4},{7,5},{8,10},{9,11},{10,... | collective-permute-start | bytes 4718600 | tf_op jit(solution)/shard_map/ppermute | solution.py:8
  211.4 1.2 copy-start
  243.0 5.7 %collective-permute-start.6 = (f32[2,4,256,384]{3,2,1,0:T(8,128)S(1)}, f32[2,4,256,384]{3,2,1,0:T(8,128)S(1)}, u32[]{:S(2)}, u32[]{:S(2)}) collective-permute-start(f32[2,4,256,384]{3,2,1,0:T(8,128)S(1)} %select_bitcast_fusion.2), channel_id=1, source_target_pairs={{0,1},{1,0},{2,3},{3,2},{4,5},{5,4},{6,7},{7,6},{8,9},{9,8},{10,11... | collective-permute-start | bytes 9437192 | tf_op jit(solution)/shard_map/ppermute | solution.py:8
  250.5 36.8 %collective-permute-start.7 = (f32[4,256,384]{2,1,0:T(8,128)}, f32[4,256,384]{2,1,0:T(8,128)}, u32[]{:S(2)}, u32[]{:S(2)}) collective-permute-start(f32[4,256,384]{2,1,0:T(8,128)} %select_bitcast_fusion.5), channel_id=1, source_target_pairs={{0,2},{1,3},{2,0},{3,1},{4,6},{5,7},{6,4},{7,5},{8,10},{9,11},{10,... | collective-permute-start | bytes 4718600 | tf_op jit(solution)/shard_map/ppermute | solution.py:8
  309.8 69.4 %collective-permute-start.8 = (f32[2,4,256,384]{3,2,1,0:T(8,128)S(1)}, f32[2,4,256,384]{3,2,1,0:T(8,128)S(1)}, u32[]{:S(2)}, u32[]{:S(2)}) collective-permute-start(f32[2,4,256,384]{3,2,1,0:T(8,128)S(1)} %select_bitcast_fusion.1), channel_id=1, source_target_pairs={{0,4},{1,5},{2,6},{3,7},{4,0},{5,1},{6,2},{7,3},{8,12},{9,13},{10,... | collective-permute-start | bytes 9437192 | tf_op jit(solution)/shard_map/ppermute | solution.py:8
  381.0 69.6 %collective-permute-start.9 = (f32[4,256,384]{2,1,0:T(8,128)}, f32[4,256,384]{2,1,0:T(8,128)}, u32[]{:S(2)}, u32[]{:S(2)}) collective-permute-start(f32[4,256,384]{2,1,0:T(8,128)} %select_bitcast_fusion.4), channel_id=1, source_target_pairs={{0,8},{1,9},{2,10},{3,11},{4,12},{5,13},{6,14},{7,15},{8,0},{9,1},... | collective-permute-start | bytes 4718600 | tf_op jit(solution)/shard_map/ppermute | solution.py:8
  473.8 5.7 %collective-permute-start.10 = (f32[2,4,256,384]{3,2,1,0:T(8,128)S(1)}, f32[2,4,256,384]{3,2,1,0:T(8,128)S(1)}, u32[]{:S(2)}, u32[]{:S(2)}) collective-permute-start(f32[2,4,256,384]{3,2,1,0:T(8,128)S(1)} %select_bitcast_fusion), channel_id=1, source_target_pairs={{0,1},{1,0},{2,3},{3,2},{4,5},{5,4},{6,7},{7,6},{8,9},{9,8},{10,11... | collective-permute-start | bytes 9437192 | tf_op jit(solution)/shard_map/ppermute | solution.py:8
  481.3 36.8 %collective-permute-start.11 = (f32[4,256,384]{2,1,0:T(8,128)}, f32[4,256,384]{2,1,0:T(8,128)}, u32[]{:S(2)}, u32[]{:S(2)}) collective-permute-start(f32[4,256,384]{2,1,0:T(8,128)} %select_bitcast_fusion.3), channel_id=1, source_target_pairs={{0,2},{1,3},{2,0},{3,1},{4,6},{5,7},{6,4},{7,5},{8,10},{9,11},{10,... | collective-permute-start | bytes 4718600 | tf_op jit(solution)/shard_map/ppermute | solution.py:8
